TPU v7x, 32 devices: a whole 2x2x4 slice. The times are simulated.
32 devices in a mesh: groups: 2 (over x), tensor: 16 (over z, y, core).
Axes of the slice: x: 2, y: 2, z: 4, core: 2. Of those that a mesh axis runs over, the one named last changes fastest.
Arguments:
- stem_field: float32 [8, 2, 262144], P('groups', None, 'tensor'), parts along dimension 0, may hold values from -6 to 6
- branches: float32 [4, 2, 2, 256, 256], P(None, None, None, None, 'tensor'), may hold values from -0.25 to 0.25
- branch_order: int32 [4], replicated, may hold values from 0 to 3, each once
- slice_values: int32 [8, 4], P('groups'), parts along dimension 0, may hold values from 0 to 1
Outputs:
- amplitudes: float32 [4, 262144], P('groups', 'tensor'), parts along dimension 0
There are 2 independent parts, one for each index of `groups`. A program takes and returns all parts, laid end to end along the dimension named above; an argument that names none is the same for every part. Nothing has to cross between parts.
Inputs may be any that keep to these rules, and one draw needn't show every extreme that they name: `branch_order`: each branch is merged exactly once.
All inputs are finite; a program needn't handle non-finite values.
Results may differ from a plain program's by a relative error of at most 0.00014.
Values sent between devices are 32-bit elements; how exact they have to be, the bound alone decides.
A program may use at most 64 MiB of HBM per device.

v0:
```python
import functools

import jax
import jax.numpy as jnp
from jax import lax
from jax.experimental import pallas as pl
from jax.experimental.pallas import tpu as pltpu
from jax.sharding import PartitionSpec as P

MESH = pl.DeviceIdType.MESH


def product(left, right):
    return jnp.einsum("smi,sil->slm", left, right, precision=lax.Precision.HIGHEST)


def combine_branch(stem_part, branch_now, values_now):
    slices, _, _, width = stem_part.shape
    chosen = jnp.where(
        (values_now == 1)[:, None, None, None], branch_now[1][None], branch_now[0][None]
    )
    real_part = product(stem_part[:, 0], chosen[:, 0]) - product(stem_part[:, 1], chosen[:, 1])
    imag_part = product(stem_part[:, 0], chosen[:, 1]) + product(stem_part[:, 1], chosen[:, 0])
    return jnp.stack([real_part, imag_part], axis=1)


def plain_device(stem_field, branches, branch_order, slice_values):
    shards = lax.axis_size("tensor")
    steps = branches.shape[0]
    width = branches.shape[3]
    current = stem_field
    for step in range(steps):
        table = lax.all_gather(
            lax.dynamic_index_in_dim(branches, branch_order[step], 0, keepdims=False),
            "tensor",
            axis=3,
            tiled=True,
        )
        slices, parts, entries = current.shape
        blocks = current.reshape(slices, parts, entries // width, width)
        combined = combine_branch(blocks, table, slice_values[:, step])
        combined = combined.reshape(slices, parts, shards, width // shards, entries // width)
        current = lax.all_to_all(
            combined, "tensor", split_axis=2, concat_axis=2, tiled=True
        ).reshape(current.shape)
    return jnp.sum(current, axis=0)


def split(value):
    high = value.astype(jnp.bfloat16)
    return high, (value - high.astype(jnp.float32)).astype(jnp.bfloat16)


def kernel(cfg, values, stem, shard, out, g0, g1, g2, g3, w0, w1, w2, w3, y, sent, got, fsent, fgot, turned_f,
           gather_sem, send_sem, x_sem, f_sem, xs_sem, fs_sem):
    T, S, K, CB, M, CLO, CHI = cfg
    Z = T // 4
    gs = (g0, g1, g2, g3)
    ws = (w0, w1, w2, w3)
    gx = lax.axis_index("groups")
    me = lax.axis_index("tensor")
    core = lax.rem(me, 2)
    col = lax.rem(me // 2, 2)
    depth = me // 4
    partner = me + 1 - 2 * core
    across_y = me + 2 - 4 * col

    barrier = pltpu.get_barrier_semaphore()
    for d in range(1, T):
        pl.semaphore_signal(barrier, inc=1, device_id=(gx, lax.rem(me + d, T)), device_id_type=MESH)
    pl.semaphore_signal(barrier, inc=1, device_id=(1 - gx, me), device_id_type=MESH)
    pl.semaphore_wait(barrier, T)

    started = []
    counter = [0] * 4
    ours = pl.ds(2 * gx, 2)
    theirs = pl.ds(2 - 2 * gx, 2)
    far = pl.ds(1, Z - 1)

    def push(src, dst, ssem, rsem, device):
        copy = pltpu.make_async_remote_copy(
            src_ref=src, dst_ref=dst, send_sem=ssem, recv_sem=rsem,
            device_id=device, device_id_type=MESH,
        )
        copy.start()
        started.append(copy)

    def arrived(dst, rsem):
        pltpu.make_async_remote_copy(
            src_ref=dst, dst_ref=dst, send_sem=rsem, recv_sem=rsem,
            device_id=(gx, partner), device_id_type=MESH).wait_recv()

    def token(t):
        counter[t] += 1
        return send_sem.at[t, counter[t] - 1]

    def send(t, src, dst, slot, device):
        push(src, dst, token(t), gather_sem.at[t, slot], device)

    def pair(t, row, levels, part, slot):
        send(t, gs[t].at[0, row, levels, part], gs[t].at[1, row, levels, part], slot, (gx, partner))

    def side(t, row, slot):
        src = gs[t].at[0, row, far, ours]
        send(t, src, src, slot, (1 - gx, me))

    def launch(t):
        for d in range(1, Z):
            to = lax.rem(depth + d, Z) * 4 + lax.rem(me, 4)
            send(t, shard.at[t, ours], gs[t].at[0, 0, Z - d, ours], 11 + Z - d, (gx, to))

    def lead(t):
        send(t, shard.at[t], gs[t].at[0, 1, 0], 0, (gx, across_y))
        send(t, shard.at[t], gs[t].at[1, 0, 0], 5, (gx, partner))

    def first(t):
        for d in range(1, Z):
            arrived(gs[t].at[0, 0, d, ours], gather_sem.at[t, 11 + d])
        send(t, gs[t].at[0, 0, far, ours], gs[t].at[0, 1, far, ours], 1, (gx, across_y))
        side(t, 0, 2)
        pair(t, 0, far, ours, 6)
        if t < 2:
            launch(t + 2)
            lead(t + 2)

    def second(t):
        arrived(gs[t].at[0, 1, far, ours], gather_sem.at[t, 1])
        side(t, 1, 3)
        pair(t, 1, far, ours, 7)
        arrived(gs[t].at[0, 1, 0], gather_sem.at[t, 0])
        send(t, gs[t].at[0, 1, 0], gs[t].at[1, 1, 0], 8, (gx, partner))

    def third(t):
        arrived(gs[t].at[0, 0, far, theirs], gather_sem.at[t, 2])
        pair(t, 0, far, theirs, 9)
        arrived(gs[t].at[0, 1, far, theirs], gather_sem.at[t, 3])
        pair(t, 1, far, theirs, 10)

    def settle(t):
        arrived(gs[t].at[1, 0, 0], gather_sem.at[t, 5])
        arrived(gs[t].at[1, 0, far, ours], gather_sem.at[t, 6])
        arrived(gs[t].at[1, 1, far, ours], gather_sem.at[t, 7])
        arrived(gs[t].at[1, 1, 0], gather_sem.at[t, 8])
        arrived(gs[t].at[1, 0, far, theirs], gather_sem.at[t, 9])
        arrived(gs[t].at[1, 1, far, theirs], gather_sem.at[t, 10])

    def load_tables(t):
        settle(t)
        g, w = gs[t], ws[t]
        for a in range(T):
            z, c, which = a // 4, (a // 2) % 2, a % 2
            rel = lax.rem(z - depth + Z, Z)
            row = jnp.where(col == c, 0, 1)
            other = jnp.where(core == which, 0, 1)
            for v in range(2):
                for p in range(2):
                    high, low = split(g[other, row, rel, 2 * v + p])
                    rows = slice(a * K, (a + 1) * K)
                    cols = slice(p * CB, (p + 1) * CB)
                    w[v, 0, rows, cols] = high
                    w[v, 1, rows, cols] = low
        if t >= 2 and CHI > 1:
            row = lax.broadcasted_iota(jnp.int32, (CB, CB), 0)
            lane = lax.broadcasted_iota(jnp.int32, (CB, CB), 1)
            if t == 2:
                c, lo, h = lane // (CLO * T), (lane // T) % CLO, lane % T
            else:
                lo, c, h = lane // (CHI * T), (lane // T) % CHI, lane % T
            move = (row == (lo * T + h) * CHI + c).astype(jnp.float32).astype(jnp.bfloat16)
            for v in range(2):
                for i in range(2):
                    for p in range(2):
                        cols = slice(p * CB, (p + 1) * CB)
                        w[v, i, :, cols] = jnp.dot(
                            w[v, i, :, cols], move, preferred_element_type=jnp.float32
                        ).astype(jnp.bfloat16)

    def merge(t, v, real, imag):
        rh, rl = split(real)
        ih, il = split(imag)
        ah = jnp.concatenate([jnp.concatenate([rh, -ih], axis=1), jnp.concatenate([ih, rh], axis=1)], axis=0)
        al = jnp.concatenate([jnp.concatenate([rl, -il], axis=1), jnp.concatenate([il, rl], axis=1)], axis=0)
        dims = (((1,), (1,)), ((), ()))
        dot = functools.partial(lax.dot_general, dimension_numbers=dims,
                                preferred_element_type=jnp.float32)
        wh, wl = ws[t][v, 0], ws[t][v, 1]
        return dot(wh, ah) + (dot(wh, al) + dot(wl, ah))

    def regroup(ref, chi_major):
        rows = CB // CLO
        pieces = []
        for lo in range(CLO):
            if chi_major:
                pieces.append(jnp.concatenate(
                    [ref[pl.ds(c * CLO + lo, T, stride=K), :] for c in range(CHI)], axis=0))
            else:
                pieces.append(ref[pl.ds(lo, rows, stride=CLO), :])
        return [jnp.concatenate([b[:, p * M:(p + 1) * M] for b in pieces], axis=1) for p in range(2)]

    for t in range(2):
        launch(t)
    lead(0)
    lead(1)
    pending = [(first, 0), (first, 1), (second, 0), (second, 1), (third, 0), (first, 2), (third, 1),
               (first, 3), (second, 2), (second, 3), (third, 2), (third, 3)]

    def more(count):
        for _ in range(min(count, len(pending))):
            action, t = pending.pop(0)
            action(t)

    more(5)
    for t in range(4):
        gs[t][0, 0, 0] = shard[t]
    load_tables(0)
    for s in range(S):
        y[s] = merge(0, values[s, 0], stem[s, 0], stem[s, 1])
        if s % 2:
            more(1)
    load_tables(1)
    rows_of = lambda s, i: pl.ds(pl.multiple_of((s * T + i) * K, K), K)
    for s in range(S):
        real, imag = regroup(y.at[s], True)
        sent[pl.ds(s * T * K, T * K), :] = merge(1, values[s, 1], real, imag)
        for d in range(1, T):
            to = lax.rem(me + d, T)
            push(sent.at[rows_of(s, to)], got.at[rows_of(s, me)], xs_sem.at[s, d], x_sem.at[s, d], (gx, to))
        got[rows_of(s, me), :] = sent[rows_of(s, me), :]
        more(1)
    more(len(pending))
    load_tables(2)
    load_tables(3)
    sums = [None, None]
    for s in range(S):
        for d in range(1, T):
            frm = lax.rem(me - d + T, T)
            arrived(got.at[rows_of(s, frm)], x_sem.at[s, d])
        parts = [[], []]
        for hi in range(CHI):
            block = jnp.concatenate(
                [got[pl.ds(s * T * K + hi * CLO + lo, T, stride=K), :] for lo in range(CLO)], axis=0)
            turned = block.T
            for p in range(2):
                parts[p].append(jnp.concatenate(
                    [turned[(p * CHI + c) * T:(p * CHI + c + 1) * T] for c in range(CHI)], axis=1))
        real, imag = [jnp.concatenate(q, axis=0) for q in parts]
        r = merge(2, values[s, 2], real, imag)
        one = values[s, 3] == 1
        for v in range(2):
            part = jnp.where(one if v else jnp.logical_not(one), r, 0.0)
            sums[v] = part if s == 0 else sums[v] + part
    y[0] = sums[0]
    y[1] = sums[1]
    total = None
    for v in range(2):
        real, imag = regroup(y.at[v], False)
        r = merge(3, v, real, imag)
        total = r if v == 0 else total + r
    fsent[...] = total
    row_of = lambda i: pl.ds(pl.multiple_of(i * K, K), K)
    for d in range(1, T):
        to = lax.rem(me + d, T)
        push(fsent.at[row_of(to)], fgot.at[row_of(me)], fs_sem.at[d], f_sem.at[d], (gx, to))
    fgot[row_of(me), :] = fsent[row_of(me), :]
    for d in range(1, T):
        frm = lax.rem(me - d + T, T)
        arrived(fgot.at[row_of(frm)], f_sem.at[d])

    lanes = 2 * M
    width = lanes // CHI
    across = jnp.concatenate([fgot[pl.ds(c, T, stride=K), :] for c in range(K)], axis=0)
    halves = CB // lanes
    for i in range(halves):
        turned_f[i] = across[i * lanes:(i + 1) * lanes].T
    pieces = [jnp.concatenate(
        [turned_f[i, pl.ds(c, 2 * T, stride=CHI), :] for i in range(halves)], axis=1) for c in range(CHI)]
    count = CB // width
    lined = jnp.concatenate(
        [jnp.concatenate([q[:, j * width:(j + 1) * width] for q in pieces], axis=1) for j in range(count)], axis=0)
    row = lax.broadcasted_iota(jnp.int32, (lanes, lanes), 0)
    lane = lax.broadcasted_iota(jnp.int32, (lanes, lanes), 1)
    move = (row == (lane % CHI) * width + lane // CHI).astype(jnp.float32).astype(jnp.bfloat16)
    first, rest = lined.astype(jnp.bfloat16), lined
    rest = rest - first.astype(jnp.float32)
    second, third = split(rest)
    dot = functools.partial(jnp.dot, preferred_element_type=jnp.float32)
    placed = (dot(first, move) + dot(second, move)) + dot(third, move)
    for j in range(count):
        out[:, j * lanes:(j + 1) * lanes] = placed[j * 2 * T:(j + 1) * 2 * T]
    for copy in started:
        copy.wait_send()


def fused_device(stem_field, branches, branch_order, slice_values):
    T = lax.axis_size("tensor")
    S, _, entries = stem_field.shape
    steps, _, _, CB, K = branches.shape
    M = entries // CB
    CLO = CB // M
    CHI = K // CLO
    stem = stem_field.reshape(S, 2, M, CB)
    shard = branches.at[branch_order].get(mode="promise_in_bounds").reshape(steps, 4, CB, K).transpose(0, 1, 3, 2)
    vmem = pl.BlockSpec(memory_space=pltpu.VMEM)
    dma = pltpu.SemaphoreType.DMA
    table = pltpu.VMEM((2, 2, T // 4, 4, K, CB), jnp.float32)
    merged = pltpu.VMEM((2, 2, CB, 2 * CB), jnp.bfloat16)
    moved = pltpu.VMEM((T * S * K, 2 * M), jnp.float32)
    gathered = pl.pallas_call(
        functools.partial(kernel, (T, S, K, CB, M, CLO, CHI)),
        out_shape=jax.ShapeDtypeStruct((2 * T, entries // T), jnp.float32),
        in_specs=[pl.BlockSpec(memory_space=pltpu.SMEM), vmem, vmem],
        out_specs=vmem,
        scratch_shapes=[
            table, table, table, table,
            merged, merged, merged, merged,
            pltpu.VMEM((S, CB, 2 * M), jnp.float32),
            moved, moved,
            pltpu.VMEM((CB, 2 * M), jnp.float32),
            pltpu.VMEM((CB, 2 * M), jnp.float32),
            pltpu.VMEM((CB // (2 * M), 2 * M, 2 * M), jnp.float32),
            dma((4, 11 + T // 4)), dma((4, 11 + T // 4)),
            dma((S, T)), dma((T,)), dma((S, T)), dma((T,)),
        ],
        compiler_params=pltpu.CompilerParams(collective_id=0, has_side_effects=True),
    )(slice_values, stem, shard)
    return gathered.reshape(2, entries)


def solution(mesh):
    def per_device(stem_field, branches, branch_order, slice_values):
        shards = lax.axis_size("tensor")
        steps, _, _, width, columns = branches.shape
        middle = stem_field.shape[2] // width
        fits = (
            mesh.shape["groups"] == 2 and shards % 8 == 0 and columns % 8 == 0 and steps == 4
            and 2 * middle == 128 and width % middle == 0 and columns % (width // middle) == 0
        )
        run = fused_device if fits else plain_device
        return run(stem_field, branches, branch_order, slice_values)

    return jax.shard_map(
        per_device,
        mesh=mesh,
        in_specs=(
            P("groups", None, "tensor"),
            P(None, None, None, None, "tensor"),
            P(),
            P("groups", None),
        ),
        out_specs=P("groups", "tensor"),
        check_vma=False,
    )
```

profile of v0, /device:TPU:0, one launch (start us, length us, event | category | flops | bytes accessed | tf_op | source)
XLA Modules:
  0.0 55.0 jit_solution(1221769379140632125)
XLA Ops:
  0.0 0.0 copy-start
  0.0 0.7 %compare_select_fusion = s32[4]{0:T(128)S(1)} fusion(s32[4]{0:T(128)} %param.6), kind=kLoop, calls=%fused_computation.2 | loop fusion | flops 12 | bytes 32 | tf_op jit(solution)/shard_map/select_n | solution.py:302
  0.7 0.3 copy-done
  1.0 0.0 copy-start.1
  1.0 1.2 %gather_fusion = f32[4,2,2,256,16]{3,4,2,1,0:T(8,128)} fusion(f32[4,2,2,256,16]{3,4,2,1,0:T(8,128)S(1)} %copy-done, s32[1024]{0:T(1024)S(1)} %pad_clamp_fusion), kind=kCustom, calls=%fused_computation | custom fusion | bytes 524304 | tf_op jit(solution)/shard_map/gather | solution.py:302
  2.2 0.0 copy-done.1
  2.2 1.2 %reshape.9.stem = f32[4,2,64,256]{3,2,1,0:T(8,128)} reshape(f32[4,2,16384]{2,1,0:T(2,128)S(1)} %copy-done.1) | data formatting | bytes 1048576 | tf_op jit(solution)/shard_map/reshape | solution.py:301
  3.5 49.8 %shard_map.46 = f32[32,1024]{1,0:T(8,128)} custom-call(s32[4,4]{1,0:T(4,128)} %values.1, f32[4,2,64,256]{3,2,1,0:T(8,128)} %reshape.9.stem, f32[4,4,16,256]{3,2,1,0:T(8,128)} %bitcast.3), custom_call_target="tpu_custom_call" | custom-call | tf_op jit(solution)/shard_map/pallas_call | solution.py:308
  53.3 1.7 %reshape.11 = f32[2,16384]{1,0:T(2,128)} reshape(f32[32,1024]{1,0:T(8,128)} %shard_map.46) | data formatting | bytes 262144 | tf_op jit(solution)/shard_map/reshape | solution.py:326
  (1 shorter events, 0.0 us)
Async XLA Ops:
  0.0 1.0 %copy-start = (f32[4,2,2,256,16]{3,4,2,1,0:T(8,128)S(1)}, f32[4,2,2,256,16]{3,4,2,1,0:T(8,128)}, u32[]{:S(2)}) copy-start(f32[4,2,2,256,16]{3,4,2,1,0:T(8,128)} %param.5) | copy-start | bytes 786436
  1.0 1.3 %copy-start.1 = (f32[4,2,16384]{2,1,0:T(2,128)S(1)}, f32[4,2,16384]{2,1,0:T(2,128)}, u32[]{:S(2)}) copy-start(f32[4,2,16384]{2,1,0:T(2,128)} %param.4) | copy-start | bytes 1572868
where the time goes:
time: 55.1 us; the launch traced here: 55 us
  Pallas kernels  49.8 us (90%)
  local copies, waits for them, and re-layouts  4.41 us (8%)
  other arithmetic  0.71 us (1%)
    pallas_call x1, Pallas kernels, fused_device(): pl.pallas_call(functools.partial(kernel, (T, S, K, CB, M, CLO, CHI)), out...  49.8 us
    reshape x1, local copies, waits for them, and re-layouts, fused_device(): return gathered.reshape(2, entries)  1.67 us
    gather x1, local copies, waits for them, and re-layouts, fused_device(): branches.at[branch_order].get(mode='promise_in_bounds')  1.25 us
    reshape x1, local copies, waits for them, and re-layouts, fused_device(): stem = stem_field.reshape(S, 2, M, CB)  1.23 us

commit v1 on v0

--- a/solution.py
+++ b/solution.py
@@ -51,8 +51,8 @@
     return high, (value - high.astype(jnp.float32)).astype(jnp.bfloat16)
 
 
-def kernel(cfg, values, stem, shard, out, g0, g1, g2, g3, w0, w1, w2, w3, y, sent, got, fsent, fgot, turned_f,
-           gather_sem, send_sem, x_sem, f_sem, xs_sem, fs_sem):
+def kernel(cfg, order, values, stem_hbm, branches_hbm, out, stem, table, shard, g0, g1, g2, g3, w0, w1, w2, w3, y, sent, got, fsent, fgot, turned_f,
+           gather_sem, send_sem, x_sem, f_sem, xs_sem, fs_sem, in_sem):
     T, S, K, CB, M, CLO, CHI = cfg
     Z = T // 4
     gs = (g0, g1, g2, g3)
@@ -65,10 +65,17 @@
     partner = me + 1 - 2 * core
     across_y = me + 2 - 4 * col
 
+    load_branches = pltpu.make_async_copy(branches_hbm, table, in_sem.at[0])
+    load_branches.start()
+    load_stem = pltpu.make_async_copy(stem_hbm, stem, in_sem.at[1])
+    load_stem.start()
     barrier = pltpu.get_barrier_semaphore()
     for d in range(1, T):
         pl.semaphore_signal(barrier, inc=1, device_id=(gx, lax.rem(me + d, T)), device_id_type=MESH)
     pl.semaphore_signal(barrier, inc=1, device_id=(1 - gx, me), device_id_type=MESH)
+    load_branches.wait()
+    for t in range(4):
+        shard[t] = table[order[t]]
     pl.semaphore_wait(barrier, T)
 
     started = []
@@ -175,6 +182,12 @@
                             w[v, i, :, cols], move, preferred_element_type=jnp.float32
                         ).astype(jnp.bfloat16)
 
+    def stem_part(s, p):
+        lanes = 2 * M
+        pieces = CB // lanes
+        return jnp.concatenate(
+            [stem[s, pl.ds(2 * i + p, M, stride=2 * pieces), :] for i in range(pieces)], axis=1)
+
     def merge(t, v, real, imag):
         rh, rl = split(real)
         ih, il = split(imag)
@@ -213,8 +226,9 @@
     for t in range(4):
         gs[t][0, 0, 0] = shard[t]
     load_tables(0)
+    load_stem.wait()
     for s in range(S):
-        y[s] = merge(0, values[s, 0], stem[s, 0], stem[s, 1])
+        y[s] = merge(0, values[s, 0], stem_part(s, 0), stem_part(s, 1))
         if s % 2:
             more(1)
     load_tables(1)
@@ -286,7 +300,8 @@
     dot = functools.partial(jnp.dot, preferred_element_type=jnp.float32)
     placed = (dot(first, move) + dot(second, move)) + dot(third, move)
     for j in range(count):
-        out[:, j * lanes:(j + 1) * lanes] = placed[j * 2 * T:(j + 1) * 2 * T]
+        for p in range(2):
+            out[pl.ds(2 * j + p, T, stride=2 * count), :] = placed[(2 * j + p) * T:(2 * j + p + 1) * T]
     for copy in started:
         copy.wait_send()
 
@@ -298,20 +313,24 @@
     M = entries // CB
     CLO = CB // M
     CHI = K // CLO
-    stem = stem_field.reshape(S, 2, M, CB)
-    shard = branches.at[branch_order].get(mode="promise_in_bounds").reshape(steps, 4, CB, K).transpose(0, 1, 3, 2)
+    lanes = 2 * M
+    stem = stem_field.reshape(S, 2, entries // lanes, lanes).transpose(0, 2, 1, 3).reshape(S, 2 * entries // lanes, lanes)
+    table = branches.reshape(steps, 4, CB, K).transpose(0, 1, 3, 2)
     vmem = pl.BlockSpec(memory_space=pltpu.VMEM)
+    smem = pl.BlockSpec(memory_space=pltpu.SMEM)
+    hbm = pl.BlockSpec(memory_space=pltpu.HBM)
     dma = pltpu.SemaphoreType.DMA
-    table = pltpu.VMEM((2, 2, T // 4, 4, K, CB), jnp.float32)
+    gathers = pltpu.VMEM((2, 2, T // 4, 4, K, CB), jnp.float32)
     merged = pltpu.VMEM((2, 2, CB, 2 * CB), jnp.bfloat16)
     moved = pltpu.VMEM((T * S * K, 2 * M), jnp.float32)
     gathered = pl.pallas_call(
         functools.partial(kernel, (T, S, K, CB, M, CLO, CHI)),
-        out_shape=jax.ShapeDtypeStruct((2 * T, entries // T), jnp.float32),
-        in_specs=[pl.BlockSpec(memory_space=pltpu.SMEM), vmem, vmem],
+        out_shape=jax.ShapeDtypeStruct((2 * entries // lanes, lanes), jnp.float32),
+        in_specs=[smem, smem, hbm, hbm],
         out_specs=vmem,
         scratch_shapes=[
-            table, table, table, table,
+            pltpu.VMEM(stem.shape, jnp.float32), pltpu.VMEM(table.shape, jnp.float32), pltpu.VMEM(table.shape, jnp.float32),
+            gathers, gathers, gathers, gathers,
             merged, merged, merged, merged,
             pltpu.VMEM((S, CB, 2 * M), jnp.float32),
             moved, moved,
@@ -319,11 +338,11 @@
             pltpu.VMEM((CB, 2 * M), jnp.float32),
             pltpu.VMEM((CB // (2 * M), 2 * M, 2 * M), jnp.float32),
             dma((4, 11 + T // 4)), dma((4, 11 + T // 4)),
-            dma((S, T)), dma((T,)), dma((S, T)), dma((T,)),
+            dma((S, T)), dma((T,)), dma((S, T)), dma((T,)), dma((2,)),
         ],
         compiler_params=pltpu.CompilerParams(collective_id=0, has_side_effects=True),
-    )(slice_values, stem, shard)
-    return gathered.reshape(2, entries)
+    )(branch_order, slice_values, stem, table)
+    return gathered.reshape(entries // lanes, 2, lanes).transpose(1, 0, 2).reshape(2, entries)
 
 
 def solution(mesh):

time: 55.1 us -> 51.3 us (0.931)
  local copies, waits for them, and re-layouts: 4.41 us -> 1.57 us
  other arithmetic: 0.71 us -> 0 us
    reshape x2 -> x0, local copies, waits for them, and re-layouts: 2.9 us -> none  [the longest x1 1.67 us: fused_device(): return gathered.reshape(2, entries)]
    unnamed x4 -> x1, local copies, waits for them, and re-layouts: 0.26 us -> 1.57 us
    gather x1 -> x0, local copies, waits for them, and re-layouts: 1.25 us -> none  [fused_device(): branches.at[branch_order].get(mode='promise_in_bounds')]
    select_n x1 -> x0, other arithmetic: 0.7 us -> none  [fused_device(): branches.at[branch_order].get(mode='promise_in_bounds')]
where the time goes in v1:
time: 51.3 us; the launch traced here: 51.1 us
  Pallas kernels  49.5 us (96%)
  local copies, waits for them, and re-layouts  1.57 us (3%)
    pallas_call x1, Pallas kernels, fused_device(): pl.pallas_call(functools.partial(kernel, (T, S, K, CB, M, CLO, CHI)), out...  49.5 us
    unnamed x1, local copies, waits for them, and re-layouts  1.57 us

profile of v1, /device:TPU:0, one launch (start us, length us, event | category | flops | bytes accessed | tf_op | source)
XLA Modules:
  0.0 51.1 jit_solution(1693057757664466481)
XLA Ops:
  0.0 49.5 %shard_map.46 = f32[256,128]{1,0:T(8,128)} custom-call(s32[4]{0:T(128)} %order.1, s32[4,4]{1,0:T(4,128)} %values.1, f32[4,256,128]{2,1,0:T(8,128)} %bitcast.14, f32[4,4,16,256]{3,2,1,0:T(8,128)} %bitcast.15), custom_call_target="tpu_custom_call" | custom-call | tf_op jit(solution)/shard_map/pallas_call | solution.py:326
  49.5 1.6 %copy.8 = f32[2,16384]{1,0:T(2,128)} copy(f32[2,16384]{1,0:T(2,128)} %bitcast.13) | data formatting | bytes 262144

commit v2 on v1

v2 whole, which is shorter than its diff:
```python
import functools

import jax
import jax.numpy as jnp
from jax import lax
from jax.experimental import pallas as pl
from jax.experimental.pallas import tpu as pltpu
from jax.sharding import PartitionSpec as P

MESH = pl.DeviceIdType.MESH
scope = jax.named_scope


def product(left, right):
    return jnp.einsum("smi,sil->slm", left, right, precision=lax.Precision.HIGHEST)


def combine_branch(stem_part, branch_now, values_now):
    slices, _, _, width = stem_part.shape
    chosen = jnp.where(
        (values_now == 1)[:, None, None, None], branch_now[1][None], branch_now[0][None]
    )
    real_part = product(stem_part[:, 0], chosen[:, 0]) - product(stem_part[:, 1], chosen[:, 1])
    imag_part = product(stem_part[:, 0], chosen[:, 1]) + product(stem_part[:, 1], chosen[:, 0])
    return jnp.stack([real_part, imag_part], axis=1)


def plain_device(stem_field, branches, branch_order, slice_values):
    shards = lax.axis_size("tensor")
    steps = branches.shape[0]
    width = branches.shape[3]
    current = stem_field
    for step in range(steps):
        table = lax.all_gather(
            lax.dynamic_index_in_dim(branches, branch_order[step], 0, keepdims=False),
            "tensor",
            axis=3,
            tiled=True,
        )
        slices, parts, entries = current.shape
        blocks = current.reshape(slices, parts, entries // width, width)
        combined = combine_branch(blocks, table, slice_values[:, step])
        combined = combined.reshape(slices, parts, shards, width // shards, entries // width)
        current = lax.all_to_all(
            combined, "tensor", split_axis=2, concat_axis=2, tiled=True
        ).reshape(current.shape)
    return jnp.sum(current, axis=0)


def split(value):
    high = value.astype(jnp.bfloat16)
    return high, (value - high.astype(jnp.float32)).astype(jnp.bfloat16)


def flip(index, mask):
    bit = 1
    while bit <= mask:
        if mask & bit:
            index = index + bit * (1 - 2 * lax.rem(index // bit, 2))
        bit *= 2
    return index


def kernel(cfg, order, values, stem_hbm, branches_hbm, out_hbm, stem, table, out, g0, g1, g2, g3, w0, w1, w2, w3,
           y, sent, got, fsent, fgot, turned_f, gather_sem, send_sem, x_sem, f_sem, in_sem):
    T, S, K, CB, M, CLO, CHI = cfg
    Z = T // 4
    gs = (g0, g1, g2, g3)
    ws = (w0, w1, w2, w3)
    gx = lax.axis_index("groups")
    me = lax.axis_index("tensor")
    core = lax.rem(me, 2)
    depth = me // 4

    load_branches = pltpu.make_async_copy(branches_hbm, table, in_sem.at[0])
    load_branches.start()
    load_stem = pltpu.make_async_copy(stem_hbm, stem, in_sem.at[1])
    load_stem.start()
    barrier = pltpu.get_barrier_semaphore()
    for d in range(1, T):
        pl.semaphore_signal(barrier, inc=1, device_id=(gx, lax.rem(me + d, T)), device_id_type=MESH)
    pl.semaphore_signal(barrier, inc=1, device_id=(1 - gx, me), device_id_type=MESH)
    with scope("inputs"):
        load_branches.wait()
        for t in range(4):
            gs[t][me] = table[order[t]]
    with scope("barrier"):
        pl.semaphore_wait(barrier, T)

    ours = pl.ds(2 * gx, 2)
    theirs = pl.ds(2 - 2 * gx, 2)
    both = pl.ds(0, 4)
    partner = (gx, flip(me, 1))
    beside = (gx, flip(me, 2))
    across = (1 - gx, me)

    def push(src, dst, ssem, rsem, device):
        pltpu.make_async_remote_copy(
            src_ref=src, dst_ref=dst, send_sem=ssem, recv_sem=rsem,
            device_id=device, device_id_type=MESH,
        ).start()

    def arrived(dst, rsem):
        pltpu.make_async_remote_copy(
            src_ref=dst, dst_ref=dst, send_sem=rsem, recv_sem=rsem,
            device_id=partner, device_id_type=MESH).wait_recv()

    def left(src, ssem):
        pltpu.make_async_remote_copy(
            src_ref=src, dst_ref=src, send_sem=ssem, recv_sem=ssem,
            device_id=partner, device_id_type=MESH).wait_send()

    PAIR, ZT, B = 0, 1, 2
    ZO, C, XA, XC = 2, 2 + (Z - 1), 2 + 2 * (Z - 1), 2 + 3 * (Z - 1)

    def piece(t, k, row, half):
        return gs[t].at[flip(me, 4 * k + 2 * row), half]

    def send(t, ref, slot, device):
        push(ref, ref, send_sem.at[t], gather_sem.at[t, slot], device)

    def twin(t, ref):
        send(t, ref, PAIR, partner)

    def take(t, ref, slot):
        arrived(ref, gather_sem.at[t, slot])

    def launch(t):
        for k in range(1, Z):
            send(t, piece(t, 0, 0, ours), ZO + k, (gx, flip(me, 4 * k)))

    def surplus(t):
        send(t, piece(t, 0, 0, theirs), ZT, (gx, flip(me, 4)))

    def lead(t):
        send(t, piece(t, 0, 0, both), B, beside)
        twin(t, piece(t, 0, 0, both))

    def column(t, k):
        ref = piece(t, k, 0, ours)
        take(t, ref, ZO + k)
        send(t, ref, C + k, beside)
        if k > 1:
            send(t, ref, XA + k, across)
        twin(t, ref)

    def extra(t):
        ref = piece(t, 1, 0, theirs)
        take(t, ref, ZT)
        if t < 2:
            send(t, ref, XC + 1, beside)
        twin(t, ref)

    def row(t):
        ref = piece(t, 0, 1, both)
        take(t, ref, B)
        twin(t, ref)

    def corner(t, k):
        ref = piece(t, k, 1, ours)
        take(t, ref, C + k)
        if k > 1 or t >= 2:
            send(t, ref, XC + k, across)
        twin(t, ref)

    def side(t, k):
        ref = piece(t, k, 0, theirs)
        take(t, ref, XA + k)
        twin(t, ref)

    def last(t, k):
        ref = piece(t, k, 1, theirs)
        take(t, ref, XC + k)
        twin(t, ref)

    def settle(t):
        arrived(gs[t].at[pl.ds(0, T // 2)], gather_sem.at[t, PAIR])

    def load_tables(t):
        with scope(f"settle{t}"):
            settle(t)
        g, w = gs[t], ws[t]
        for a in range(T):
            for v in range(2):
                for p in range(2):
                    high, low = split(g[a, 2 * v + p])
                    rows = slice(a * K, (a + 1) * K)
                    cols = slice(p * CB, (p + 1) * CB)
                    w[v, 0, rows, cols] = high
                    w[v, 1, rows, cols] = low
        if t >= 2 and CHI > 1:
            row = lax.broadcasted_iota(jnp.int32, (CB, CB), 0)
            lane = lax.broadcasted_iota(jnp.int32, (CB, CB), 1)
            if t == 2:
                c, lo, h = lane // (CLO * T), (lane // T) % CLO, lane % T
            else:
                lo, c, h = lane // (CHI * T), (lane // T) % CHI, lane % T
            move = (row == (lo * T + h) * CHI + c).astype(jnp.float32).astype(jnp.bfloat16)
            for v in range(2):
                for i in range(2):
                    for p in range(2):
                        cols = slice(p * CB, (p + 1) * CB)
                        w[v, i, :, cols] = jnp.dot(
                            w[v, i, :, cols], move, preferred_element_type=jnp.float32
                        ).astype(jnp.bfloat16)

    def stem_part(s, p):
        lanes = 2 * M
        pieces = CB // lanes
        return jnp.concatenate(
            [stem[s, pl.ds(2 * i + p, M, stride=2 * pieces), :] for i in range(pieces)], axis=1)

    def merge(t, v, real, imag):
        rh, rl = split(real)
        ih, il = split(imag)
        ah = jnp.concatenate([jnp.concatenate([rh, -ih], axis=1), jnp.concatenate([ih, rh], axis=1)], axis=0)
        al = jnp.concatenate([jnp.concatenate([rl, -il], axis=1), jnp.concatenate([il, rl], axis=1)], axis=0)
        dims = (((1,), (1,)), ((), ()))
        dot = functools.partial(lax.dot_general, dimension_numbers=dims,
                                preferred_element_type=jnp.float32)
        wh, wl = ws[t][v, 0], ws[t][v, 1]
        return dot(wh, ah) + (dot(wh, al) + dot(wl, ah))

    def regroup(ref, chi_major):
        rows = CB // CLO
        pieces = []
        for lo in range(CLO):
            if chi_major:
                pieces.append(jnp.concatenate(
                    [ref[pl.ds(c * CLO + lo, T, stride=K), :] for c in range(CHI)], axis=0))
            else:
                pieces.append(ref[pl.ds(lo, rows, stride=CLO), :])
        return [jnp.concatenate([b[:, p * M:(p + 1) * M] for b in pieces], axis=1) for p in range(2)]

    far = range(1, Z)
    steps_of = lambda action, t, ks: [(action, t, k) for k in ks]
    cross = lambda t: steps_of(side, t, range(2, Z)) + steps_of(last, t, far)
    pending, marks = [], []

    def plan(*groups):
        for group in groups:
            pending.extend(group)
        marks.append(len(pending))

    plan(steps_of(column, 0, far), [(launch, 2), (surplus, 2), (row, 0)],
         [step for k in far for step in ((corner, 0, k), (column, 1, k))],
         [(extra, 0), (lead, 2), (launch, 3), (surplus, 3), (extra, 1), (row, 1)],
         steps_of(side, 0, range(2, Z)), steps_of(corner, 1, far), steps_of(last, 0, far))
    plan(steps_of(column, 2, far), [(lead, 3)], steps_of(side, 1, range(2, Z)), [(last, 1, 1)])
    for k in range(2, Z):
        plan([(last, 1, k)])
    fresh = len(marks)
    for k in far:
        plan([(column, 3, k)])
    plan([(extra, 2), (row, 2)], steps_of(corner, 2, far), [(extra, 3), (row, 3)], steps_of(corner, 3, far), cross(2), cross(3))
    done = [0]

    def until(count):
        while done[0] < count:
            action, *args = pending[done[0]]
            with scope(f"{action.__name__}#{'.'.join(map(str, args))}"):
                action(*args)
            done[0] += 1

    with scope("launch"):
        for t in range(2):
            launch(t)
            lead(t)
        for t in range(2):
            surplus(t)
    until(marks[0])
    with scope("lt0"):
        load_tables(0)
    load_stem.wait()
    for s in range(S):
        with scope(f"m0#{s}"):
            y[s] = merge(0, values[s, 0], stem_part(s, 0), stem_part(s, 1))
        until(marks[min(s + 1, fresh - 1)])
    until(marks[fresh - 1])
    with scope("lt1"):
        load_tables(1)
    rows_of = lambda s, i: pl.ds(pl.multiple_of((s * T + i) * K, K), K)
    for s in range(S):
        with scope(f"m1#{s}"):
            real, imag = regroup(y.at[s], True)
            sent[pl.ds(s * T * K, T * K), :] = merge(1, values[s, 1], real, imag)
        for d in range(T - 1, 0, -1):
            to = flip(me, d)
            push(sent.at[rows_of(s, to)], got.at[rows_of(s, me)], x_sem.at[S], x_sem.at[s], (gx, to))
        got[rows_of(s, me), :] = sent[rows_of(s, me), :]
        until(marks[min(fresh + s, len(marks) - 2)])
    until(len(pending))
    with scope("lt2"):
        load_tables(2)
    with scope("lt3"):
        load_tables(3)

    def third(s):
        parts = [[], []]
        for hi in range(CHI):
            block = jnp.concatenate(
                [got[pl.ds(s * T * K + hi * CLO + lo, T, stride=K), :] for lo in range(CLO)], axis=0)
            turned = block.T
            for p in range(2):
                parts[p].append(jnp.concatenate(
                    [turned[(p * CHI + c) * T:(p * CHI + c + 1) * T] for c in range(CHI)], axis=1))
        real, imag = [jnp.concatenate(q, axis=0) for q in parts]
        return merge(2, values[s, 2], real, imag)

    sums = [None, None]
    total = None
    for s in range(S):
        if s == S - 1 and s > 0:
            with scope("early"):
                for v in range(2):
                    y[v] = sums[v]
                for v in range(2):
                    r = merge(3, v, *regroup(y.at[v], False))
                    total = r if v == 0 else total + r
        with scope(f"xwait#{s}"):
            arrived(got.at[pl.ds(s * T * K, (T - 1) * K)], x_sem.at[s])
        with scope(f"m2#{s}"):
            r = third(s)
            if s < S - 1:
                one_hot = values[s, 3] == 1
                for v in range(2):
                    part = jnp.where(one_hot if v else jnp.logical_not(one_hot), r, 0.0)
                    sums[v] = part if s == 0 else sums[v] + part
            else:
                y[2] = r
    with scope("m3"):
        r = merge(3, values[S - 1, 3], *regroup(y.at[2], False))
        fsent[...] = r if total is None else total + r
    row_of = lambda i: pl.ds(pl.multiple_of(i * K, K), K)
    for d in range(T - 1, 0, -1):
        to = flip(me, d)
        push(fsent.at[row_of(to)], fgot.at[row_of(me)], f_sem.at[1], f_sem.at[0], (gx, to))
    fgot[row_of(me), :] = fsent[row_of(me), :]
    for t in range(4):
        left(gs[t].at[pl.ds(0, 4 * Z - 1)], send_sem.at[t])
    left(sent.at[pl.ds(0, S * (T - 1) * K)], x_sem.at[S])
    with scope("fwait"):
        arrived(fgot.at[pl.ds(0, (T - 1) * K)], f_sem.at[0])

    lanes = 2 * M
    width = lanes // CHI
    across = jnp.concatenate([fgot[pl.ds(c, T, stride=K), :] for c in range(K)], axis=0)
    halves = CB // lanes
    for i in range(halves):
        turned_f[i] = across[i * lanes:(i + 1) * lanes].T
    pieces = [jnp.concatenate(
        [turned_f[i, pl.ds(c, 2 * T, stride=CHI), :] for i in range(halves)], axis=1) for c in range(CHI)]
    count = CB // width
    lined = jnp.concatenate(
        [jnp.concatenate([q[:, j * width:(j + 1) * width] for q in pieces], axis=1) for j in range(count)], axis=0)
    row = lax.broadcasted_iota(jnp.int32, (lanes, lanes), 0)
    lane = lax.broadcasted_iota(jnp.int32, (lanes, lanes), 1)
    move = (row == (lane % CHI) * width + lane // CHI).astype(jnp.float32).astype(jnp.bfloat16)
    first, rest = lined.astype(jnp.bfloat16), lined
    rest = rest - first.astype(jnp.float32)
    second, third = split(rest)
    dot = functools.partial(jnp.dot, preferred_element_type=jnp.float32)
    placed = (dot(first, move) + dot(second, move)) + dot(third, move)
    for j in range(count):
        for p in range(2):
            out[pl.ds(2 * j + p, T, stride=2 * count), :] = placed[(2 * j + p) * T:(2 * j + p + 1) * T]
    store = pltpu.make_async_copy(out, out_hbm, in_sem.at[2])
    store.start()
    left(fsent.at[pl.ds(0, (T - 1) * K)], f_sem.at[1])
    with scope("store"):
        store.wait()


def fused_device(stem_field, branches, branch_order, slice_values):
    T = lax.axis_size("tensor")
    S, _, entries = stem_field.shape
    steps, _, _, CB, K = branches.shape
    M = entries // CB
    CLO = CB // M
    CHI = K // CLO
    lanes = 2 * M
    stem = stem_field.reshape(S, 2, entries // lanes, lanes).transpose(0, 2, 1, 3).reshape(S, 2 * entries // lanes, lanes)
    table = branches.reshape(steps, 4, CB, K).transpose(0, 1, 3, 2)
    smem = pl.BlockSpec(memory_space=pltpu.SMEM)
    hbm = pl.BlockSpec(memory_space=pltpu.HBM)
    dma = pltpu.SemaphoreType.DMA
    gathers = pltpu.VMEM((T, 4, K, CB), jnp.float32)
    merged = pltpu.VMEM((2, 2, CB, 2 * CB), jnp.bfloat16)
    moved = pltpu.VMEM((T * S * K, 2 * M), jnp.float32)
    gathered = pl.pallas_call(
        functools.partial(kernel, (T, S, K, CB, M, CLO, CHI)),
        out_shape=jax.ShapeDtypeStruct((2 * entries // lanes, lanes), jnp.float32),
        in_specs=[smem, smem, hbm, hbm],
        out_specs=hbm,
        scratch_shapes=[
            pltpu.VMEM(stem.shape, jnp.float32), pltpu.VMEM(table.shape, jnp.float32),
            pltpu.VMEM((2 * entries // lanes, lanes), jnp.float32),
            gathers, gathers, gathers, gathers,
            merged, merged, merged, merged,
            pltpu.VMEM((S, CB, 2 * M), jnp.float32),
            moved, moved,
            pltpu.VMEM((CB, 2 * M), jnp.float32),
            pltpu.VMEM((CB, 2 * M), jnp.float32),
            pltpu.VMEM((CB // (2 * M), 2 * M, 2 * M), jnp.float32),
            dma((4, 2 + 4 * (T // 4))), dma((4,)), dma((S + 1,)), dma((2,)), dma((3,)),
        ],
        compiler_params=pltpu.CompilerParams(collective_id=0, has_side_effects=True),
    )(branch_order, slice_values, stem, table)
    return gathered.reshape(entries // lanes, 2, lanes).transpose(1, 0, 2).reshape(2, entries)


def solution(mesh):
    def per_device(stem_field, branches, branch_order, slice_values):
        shards = lax.axis_size("tensor")
        steps, _, _, width, columns = branches.shape
        middle = stem_field.shape[2] // width
        fits = (
            mesh.shape["groups"] == 2 and shards % 8 == 0 and shards & (shards - 1) == 0 and columns % 8 == 0 and steps == 4
            and 2 * middle == 128 and width % middle == 0 and columns % (width // middle) == 0
        )
        run = fused_device if fits else plain_device
        return run(stem_field, branches, branch_order, slice_values)

    return jax.shard_map(
        per_device,
        mesh=mesh,
        in_specs=(
            P("groups", None, "tensor"),
            P(None, None, None, None, "tensor"),
            P(),
            P("groups", None),
        ),
        out_specs=P("groups", "tensor"),
        check_vma=False,
    )
```

time: 51.3 us -> 49.2 us (0.959)
  Pallas kernels: 49.5 us -> 47.5 us
    pallas_call x1, Pallas kernels: 49.5 us -> 47.5 us  [fused_device(): pl.pallas_call(functools.partial(kernel, (T, S, K, CB, M, CLO, CHI)), out...]
where the time goes in v2:
time: 49.2 us; the launch traced here: 49 us
  Pallas kernels  47.5 us (97%)
  local copies, waits for them, and re-layouts  1.57 us (3%)
    pallas_call x1, Pallas kernels, fused_device(): pl.pallas_call(functools.partial(kernel, (T, S, K, CB, M, CLO, CHI)), out...  47.5 us
    unnamed x1, local copies, waits for them, and re-layouts  1.57 us

profile of v2, /device:TPU:0, one launch (start us, length us, event | category | flops | bytes accessed | tf_op | source)
XLA Modules:
  0.0 49.0 jit_solution(16492356937255076650)
XLA Ops:
  0.0 47.5 %shard_map.46 = f32[256,128]{1,0:T(8,128)} custom-call(s32[4]{0:T(128)} %order.1, s32[4,4]{1,0:T(4,128)} %values.1, f32[4,256,128]{2,1,0:T(8,128)} %bitcast.14, f32[4,4,16,256]{3,2,1,0:T(8,128)} %bitcast.15), custom_call_target="tpu_custom_call" | custom-call | tf_op jit(solution)/shard_map/pallas_call | solution.py:390
  47.5 1.6 %copy.8 = f32[2,16384]{1,0:T(2,128)} copy(f32[2,16384]{1,0:T(2,128)} %bitcast.13) | data formatting | bytes 262144
